TPU v7x, 32 devices: a whole 2x2x4 slice. The times are simulated.
32 devices in a mesh: slab: 32 (over z, y, x, core).
Axes of the slice: x: 2, y: 2, z: 4, core: 2. Of those that a mesh axis runs over, the one named last changes fastest.
Arguments:
- points: float32 [4, 128, 128, 64], P(None, 'slab'), may hold values from -6 to 6
- offsets_x: int32 [256], replicated, may hold values from 0 to 124, as said below
- coeffs_x: float32 [4, 256], replicated, may hold values from 0.1 to 1
- offsets_y: int32 [256], replicated, may hold values from 0 to 124, as said below
- coeffs_y: float32 [4, 256], replicated, may hold values from 0.1 to 1
- offsets_z: int32 [128], replicated, may hold values from 0 to 60, as said below
- coeffs_z: float32 [4, 128], replicated, may hold values from 0.1 to 1
Outputs:
- refined: float32 [4, 256, 256, 128], P(None, None, 'slab')
Inputs may be any that keep to these rules, and one draw needn't show every extreme that they name: offsets_x[i] lies between i // 2 - 2 and i // 2, clipped to 0 .. 124. offsets_y[i] lies between i // 2 - 2 and i // 2, clipped to 0 .. 124. offsets_z[i] lies between i // 2 - 2 and i // 2, clipped to 0 .. 60.
All inputs are finite; a program needn't handle non-finite values.
Results may differ from a plain program's by a relative error of at most 0.000073.
Values sent between devices are 32-bit elements; how exact they have to be, the bound alone decides.
A program may use at most 64 MiB of HBM per device.

v0:
```python
import jax
import jax.numpy as jnp
from jax import lax
from jax.sharding import PartitionSpec as P


def band_matrix(offsets, coeffs, width, start):
    weights = coeffs / jnp.sum(coeffs, axis=0, keepdims=True)
    columns = jnp.arange(width, dtype=jnp.int32)[None, :]
    first = (offsets - start)[:, None]
    matrix = jnp.zeros((offsets.shape[0], width), jnp.float32)
    for k in range(4):
        matrix = matrix + jnp.where(columns == first + k, weights[k][:, None], 0.0)
    return matrix


def along_x(matrix, grid):
    return jnp.einsum("ia,cayz->ciyz", matrix, grid, precision=lax.Precision.HIGHEST)


def along_y(matrix, grid):
    return jnp.einsum("jb,cibz->cijz", matrix, grid, precision=lax.Precision.HIGHEST)


def along_z(matrix, grid):
    return jnp.einsum("le,cije->cijl", matrix, grid, precision=lax.Precision.HIGHEST)


def body(points, offsets_x, coeffs_x, offsets_y, coeffs_y, offsets_z, coeffs_z):
    coarse_y = points.shape[2]
    coarse_z = points.shape[3]
    matrix_y = band_matrix(offsets_y, coeffs_y, coarse_y, 0)
    matrix_z = band_matrix(offsets_z, coeffs_z, coarse_z, 0)
    grid = along_y(matrix_y, points)
    grid = lax.all_to_all(grid, "slab", split_axis=2, concat_axis=1, tiled=True)
    matrix_x = band_matrix(offsets_x, coeffs_x, grid.shape[1], 0)
    grid = along_x(matrix_x, grid)
    return along_z(matrix_z, grid)


def solution(mesh):
    return jax.shard_map(
        body,
        mesh=mesh,
        in_specs=(P(None, "slab", None, None), P(), P(), P(), P(), P(), P()),
        out_specs=P(None, None, "slab", None),
        check_vma=False,
    )
```

profile of v0, /device:TPU:0, one launch (start us, length us, event | category | flops | bytes accessed | tf_op | source)
XLA Modules:
  0.0 67.6 jit_solution(16214703891033774522)
XLA Ops:
  0.0 0.0 copy-start
  0.0 0.8 %reduce_sum.27 = f32[256]{0:T(256)S(1)} reduce(f32[4,256]{1,0:T(4,128)} %param.11, f32[]{:T(128)} %constant.4.clone.1), dimensions={0}, to_apply=%region_0.0 | reduce | flops 768 | bytes 5124 | tf_op jit(solution)/shard_map/reduce_sum | solution.py:8
  0.8 0.7 %broadcast_divide_fusion.1 = f32[4,256]{1,0:T(4,128)S(1)} fusion(f32[4,256]{1,0:T(4,128)} %param.11, f32[256]{0:T(256)S(1)} %reduce_sum.27), kind=kLoop, calls=%fused_computation.70 | loop fusion | flops 1024 | bytes 9216 | tf_op jit(solution)/shard_map/div | solution.py:8
  1.5 0.7 %broadcast_add_fusion.5 = (s32[256]{0:T(256)S(1)}, s32[256]{0:T(256)S(1)}, s32[256]{0:T(256)S(1)}) fusion(s32[256]{0:T(256)} %param.10), kind=kLoop, calls=%fused_computation.81 | loop fusion | flops 768 | bytes 4096 | tf_op jit(solution)/shard_map/add | solution.py:13
  2.2 0.0 copy-done
  2.2 2.9 %convolution_bitcast_fusion = f32[4,4,256,64]{2,3,1,0:T(8,128)} fusion(f32[4,4,128,64]{2,3,1,0:T(8,128)S(1)} %copy-done, f32[256]{0:T(256)S(1)} %bitcast.50, s32[256]{0:T(256)S(1)} %get-tuple-element.21, f32[256]{0:T(256)S(1)} %bitcast.51, s32[256]{0:T(256)S(1)} %get-tuple-element.22, f32[256]{0:T(256)S(1)} %bitcast.52, s32[256]{0:T(256)S(1)} %get-tuple-element.20, ...), kind=kOutput, calls=%fused_computation.5 | convolution fusion | flops 403013632 | bytes 1581056 | tf_op jit(solution)/shard_map/jb,cibz->cijz/dot_general | solution.py:22
  5.1 2.3 %copy.12 = f32[4,4,256,64]{3,1,0,2:T(4,128)S(1)} copy(f32[4,4,256,64]{2,3,1,0:T(8,128)} %convolution_bitcast_fusion) | data formatting | bytes 2097152 | tf_op jit(solution)/shard_map/jb,cibz->cijz/transpose | solution.py:22
  7.4 0.0 copy-start.2
  7.4 0.0 copy-start.1
  7.4 0.0 copy-start.4
  7.4 0.0 copy-start.3
  7.4 2.9 %reshape.39 = f32[32,1,8192]{2,1,0:T(1,128)} reshape(f32[256,4,4,64]{3,2,1,0:T(4,128)S(1)} %bitcast.45) | data formatting | bytes 2097152
  10.3 7.3 %all-to-all-start = ((f32[32,1,8192]{2,1,0:T(1,128)}), f32[32,1,8192]{2,1,0:T(1,128)S(1)}, u32[]{:S(2)}, u32[]{:S(2)}) async-start(f32[32,1,8192]{2,1,0:T(1,128)} %reshape.39), calls=%async_computation | async-start | bytes 2097152 | tf_op jit(solution)/shard_map/all_to_all | solution.py:35
  17.7 0.0 copy-done.2
  17.7 0.0 copy-done.1
  17.7 0.0 copy-done.4
  17.8 0.0 copy-done.3
  17.8 26.0 %all-to-all-done = f32[32,1,8192]{2,1,0:T(1,128)S(1)} async-done(((f32[32,1,8192]{2,1,0:T(1,128)}), f32[32,1,8192]{2,1,0:T(1,128)S(1)}, u32[]{:S(2)}, u32[]{:S(2)}) %all-to-all-start) | async-done | bytes 1048608 | tf_op jit(solution)/shard_map/all_to_all | solution.py:35
  43.9 0.5 broadcast.42
  44.4 4.4 %reduce = f32[32,8192]{1,0:T(8,128)} reduce(f32[32,1,8192]{2,1,0:T(1,128)S(1)} %all-to-all-done, f32[]{:T(128)} %broadcast.42), dimensions={1}, to_apply=%all_to_all.13.reduce_sub_computation | reduce | bytes 2097156 | tf_op jit(solution)/shard_map/all_to_all | solution.py:35
  48.8 2.8 %reshape.40 = f32[256,4,4,64]{3,2,1,0:T(4,128)S(1)} reshape(f32[32,8192]{1,0:T(8,128)} %reduce) | data formatting | bytes 2097152
  51.6 0.7 %copy.23 = f32[4,4,256,64]{3,2,1,0:T(8,128)S(1)} copy(f32[4,4,256,64]{3,1,0,2:T(4,128)S(1)} %bitcast.47) | data formatting | bytes 2097152 | tf_op jit(solution)/shard_map/all_to_all | solution.py:35
  52.3 0.3 copy.14
  52.6 3.8 %fusion.2 = f32[4,8,64,256]{3,2,1,0:T(8,128)S(1)} fusion(f32[4,128,8,64]{3,2,1,0:T(8,128)S(1)} %bitcast.46, f32[256]{0:T(256)S(1)} %bitcast.54, s32[256]{0:T(256)S(1)} %get-tuple-element.18, f32[256]{0:T(256)S(1)} %bitcast.55, s32[256]{0:T(256)S(1)} %get-tuple-element.19, f32[256]{0:T(256)S(1)} %bitcast.56, s32[256]{0:T(256)S(1)} %get-tuple-element.17, ...), kind=kOutput, calls=%fused_computation.2 | convolution fusion | flops 805666816 | bytes 3153920 | tf_op jit(solution)/shard_map/ia,cayz->ciyz/dot_general | solution.py:18
  56.4 6.8 %fusion = f32[4,256,8,128]{3,1,2,0:T(8,128)S(1)} fusion(f32[4,8,64,256]{3,2,1,0:T(8,128)S(1)} %fusion.2, f32[128]{0:T(128)S(1)} %get-tuple-element.14, s32[128]{0:T(128)S(1)} %get-tuple-element.24, f32[128]{0:T(128)S(1)} %get-tuple-element.15, s32[128]{0:T(128)S(1)} %get-tuple-element.25, f32[128]{0:T(128)S(1)} %get-tuple-element.16, ...), kind=kOutput, calls=%fused_computation | convolution fusion | flops 805396480 | bytes 6295552 | tf_op jit(solution)/shard_map/le,cije->cijl/dot_general | solution.py:26
  63.1 4.4 %copy.16 = f32[4,256,8,128]{3,2,1,0:T(8,128)} copy(f32[4,256,8,128]{3,1,2,0:T(8,128)S(1)} %fusion) | data formatting | bytes 8388608 | tf_op jit(solution)/shard_map/le,cije->cijl/dot_general | solution.py:26
  (9 shorter events, 0.1 us)
Async XLA Ops:
  0.0 2.2 %copy-start = (f32[4,4,128,64]{2,3,1,0:T(8,128)S(1)}, f32[4,4,128,64]{2,3,1,0:T(8,128)}, u32[]{:S(2)}) copy-start(f32[4,4,128,64]{2,3,1,0:T(8,128)} %param.7) | copy-start | bytes 1572868
  7.4 10.3 %copy-start.2 = (f32[4,128]{1,0:T(4,128)S(1)}, f32[4,128]{1,0:T(4,128)}, u32[]{:S(2)}) copy-start(f32[4,128]{1,0:T(4,128)} %param.13) | copy-start | bytes 6148
  7.4 10.3 %copy-start.1 = (f32[4,256]{1,0:T(4,128)S(1)}, f32[4,256]{1,0:T(4,128)}, u32[]{:S(2)}) copy-start(f32[4,256]{1,0:T(4,128)} %param.9) | copy-start | bytes 12292
  7.4 10.3 %copy-start.4 = (s32[128]{0:T(128)S(1)}, s32[128]{0:T(128)}, u32[]{:S(2)}) copy-start(s32[128]{0:T(128)} %param.12) | copy-start | bytes 1540
  7.4 10.3 %copy-start.3 = (s32[256]{0:T(256)S(1)}, s32[256]{0:T(256)}, u32[]{:S(2)}) copy-start(s32[256]{0:T(256)} %param.8) | copy-start | bytes 3076
  10.3 33.5 %all-to-all-start = ((f32[32,1,8192]{2,1,0:T(1,128)}), f32[32,1,8192]{2,1,0:T(1,128)S(1)}, u32[]{:S(2)}, u32[]{:S(2)}) async-start(f32[32,1,8192]{2,1,0:T(1,128)} %reshape.39), calls=%async_computation | async-start | bytes 2097152 | tf_op jit(solution)/shard_map/all_to_all | solution.py:35
where the time goes:
time: 67.9 us; the launch traced here: 67.6 us
  waiting for transfers between devices  26 us (38%)
  local copies, waits for them, and re-layouts  14 us (21%)
  matrix products  13.5 us (20%)
  starting transfers between devices  7.32 us (11%)
  other arithmetic  6.6 us (10%)
    all_to_all x1, waiting for transfers between devices, body(): grid = lax.all_to_all(grid, 'slab', split_axis=2, concat_axis=1, tiled=True)  26 us
    all_to_all x1, starting transfers between devices, body(): grid = lax.all_to_all(grid, 'slab', split_axis=2, concat_axis=1, tiled=True)  7.32 us
    dot_general x1, matrix products, along_z(): jnp.einsum('le,cije->cijl', matrix, grid, precision=lax.Precision.HIGHEST)  6.76 us
    unnamed x12, local copies, waits for them, and re-layouts  5.72 us
    dot_general x1, local copies, waits for them, and re-layouts, along_z(): jnp.einsum('le,cije->cijl', matrix, grid, precision=lax.Precision.HIGHEST)  4.44 us
    all_to_all x1, other arithmetic, body(): grid = lax.all_to_all(grid, 'slab', split_axis=2, concat_axis=1, tiled=True)  4.4 us
    dot_general x1, matrix products, along_x(): jnp.einsum('ia,cayz->ciyz', matrix, grid, precision=lax.Precision.HIGHEST)  3.79 us
    dot_general x1, matrix products, along_y(): jnp.einsum('jb,cibz->cijz', matrix, grid, precision=lax.Precision.HIGHEST)  2.95 us
  transfers between devices with their start and end apart: 1, of which 1 were waited for; matrix products, arithmetic and copies ran while one was open for 0% of the time, Pallas kernels for 0%

commit v1 on v0

v1 whole, which is shorter than its diff:
```python
import functools

import jax
import jax.numpy as jnp
from jax import lax
from jax.experimental import pallas as pl
from jax.experimental.pallas import tpu as pltpu
from jax.sharding import PartitionSpec as P

MESH = pl.DeviceIdType.MESH
BAND = 4
REACH = BAND + 1
SPAN = BAND + 2


def flip(a, k, chips):
    out = 0
    bit = 1
    while bit < chips:
        a_bit, k_bit = (a // bit) % 2, (k // bit) % 2
        out = out + (a_bit + k_bit - 2 * a_bit * k_bit) * bit
        bit *= 2
    return out


def exchange(
    dims,
    points_ref, oy_ref, cy_ref, oz_ref, cz_ref, cx_ref,
    grid_ref, wx_ref,
    send, direct, passed, wy, rz, rz_lo, mixed,
    send_sem, recv_sem, pass_send_sem, pass_recv_sem,
):
    n, comps, xl, ny, nz, jl, mz = dims
    chips = n // 2
    pairs, lanes = points_ref.shape[0], points_ref.shape[1]
    fold = lanes // nz
    cl = jl // 2
    wide, narrow = 2 * cl + REACH, cl + REACH
    me = lax.axis_index("slab")
    chip, core = me // 2, me % 2
    partner = chip * 2 + 1 - core

    def wide_base(c):
        return jnp.clip(c * 2 * cl - 2, 0, ny - wide)

    def narrow_base(d):
        return jnp.clip(d * cl - 2, 0, ny - narrow)

    def span_base(j):
        return jnp.clip((me * jl + j) // 2 - 2, 0, ny - SPAN)

    rows_of_y = send.reshape(ny, pairs, lanes)

    barrier = pltpu.get_barrier_semaphore()
    pl.semaphore_signal(barrier, inc=1, device_id=(partner,), device_id_type=MESH)

    @pl.loop(1, chips)
    def _(k):
        other = flip(chip, k, chips) * 2 + core
        pl.semaphore_signal(barrier, inc=1, device_id=(other,), device_id_type=MESH)

    for p in range(pairs):
        send[pl.ds(p, ny, stride=pairs), :] = points_ref[p].T

    pl.semaphore_wait(barrier, chips)

    def out_copy(k):
        target = flip(chip, k, chips)
        return pltpu.make_async_remote_copy(
            src_ref=rows_of_y.at[pl.ds(wide_base(target), wide)],
            dst_ref=direct.at[k],
            send_sem=send_sem.at[k],
            recv_sem=recv_sem.at[k],
            device_id=(target * 2 + core,),
            device_id_type=MESH,
        )

    def pass_copy(k):
        skip = narrow_base(partner) - wide_base(chip)
        return pltpu.make_async_remote_copy(
            src_ref=direct.at[k, pl.ds(skip, narrow)],
            dst_ref=passed.at[k],
            send_sem=pass_send_sem.at[k],
            recv_sem=pass_recv_sem.at[k],
            device_id=(partner,),
            device_id_type=MESH,
        )

    @pl.loop(1, chips)
    def _(k):
        out_copy(k).start()

    own = pl.ds(wide_base(chip), wide)
    stay = pltpu.make_async_copy(rows_of_y.at[own], direct.at[0], recv_sem.at[0])
    stay.start()

    wx_ref[...] = cx_ref[...] / jnp.sum(cx_ref[...], axis=0, keepdims=True)
    wz = cz_ref[...] / jnp.sum(cz_ref[...], axis=0, keepdims=True)
    at = lax.broadcasted_iota(jnp.int32, (nz, mz), 0)
    first = jnp.broadcast_to(oz_ref[...], (nz, mz))
    band = jnp.zeros((nz, mz), jnp.float32)
    for k in range(BAND):
        band = band + jnp.where(at == first + k, jnp.broadcast_to(wz[k : k + 1], (nz, mz)), 0.0)
    high = band.astype(jnp.bfloat16)
    low = (band - high.astype(jnp.float32)).astype(jnp.bfloat16)
    rz[...] = jnp.zeros_like(rz)
    rz_lo[...] = jnp.zeros_like(rz_lo)
    for f in range(fold):
        rz[f * nz : (f + 1) * nz, f * mz : (f + 1) * mz] = high
        rz[lanes + f * nz : lanes + (f + 1) * nz, f * mz : (f + 1) * mz] = high
        rz_lo[f * nz : (f + 1) * nz, f * mz : (f + 1) * mz] = low
    for j in range(jl):
        coeffs = [jnp.full((pairs, lanes), cy_ref[k, me * jl + j]) for k in range(BAND)]
        total = coeffs[0] + coeffs[1] + coeffs[2] + coeffs[3]
        coeffs = [c / total for c in coeffs]
        skip = jnp.full((pairs, lanes), oy_ref[me * jl + j] - span_base(j))
        for m in range(SPAN):
            weight = jnp.zeros((pairs, lanes), jnp.float32)
            for k in range(max(0, m - SPAN + BAND), min(BAND, m + 1)):
                weight = jnp.where(skip == m - k, coeffs[k], weight)
            wy[j * SPAN + m] = weight

    def refine_y(place, load, base):
        for j in range(jl):
            row = span_base(j) - base
            acc = wy[j * SPAN] * load(row)
            for m in range(1, SPAN):
                acc = acc + wy[j * SPAN + m] * load(row + m)
            mixed[pl.ds(place * pairs * jl + j, pairs, stride=jl), :] = acc

    def refine_z(devices):
        rows = pairs * jl * len(devices)
        x = mixed[:rows]
        hi = x.astype(jnp.bfloat16)
        lo = (x - hi.astype(jnp.float32)).astype(jnp.bfloat16)
        both = jnp.concatenate([hi, lo], axis=1)
        res = jnp.dot(both, rz[...], preferred_element_type=jnp.float32)
        res = res + jnp.dot(hi, rz_lo[...], preferred_element_type=jnp.float32)
        per = pairs // comps
        for q, device in enumerate(devices):
            for p in range(pairs):
                for f in range(fold):
                    spot = (p // per, device * xl + (p % per) * fold + f)
                    top = (q * pairs + p) * jl
                    grid_ref[spot] = res[top : top + jl, f * mz : (f + 1) * mz]

    def from_direct(place, k):
        refine_y(
            place,
            lambda row: direct[k, row],
            wide_base(chip),
        )
        return flip(chip, k, chips) * 2 + core

    def from_passed(place, k):
        refine_y(
            place,
            lambda row: passed[k, row],
            narrow_base(me),
        )
        return flip(chip, k, chips) * 2 + 1 - core

    stay.wait()
    pass_copy(0).start()
    refine_z([from_direct(0, 0)])

    @pl.loop(1, chips)
    def _(k):
        out_copy(k).wait_recv()
        pass_copy(k).start()
        one = from_direct(0, k)
        pass_copy(k - 1).wait_recv()
        two = from_passed(1, k - 1)
        refine_z([one, two])

    pass_copy(chips - 1).wait_recv()
    refine_z([from_passed(0, chips - 1)])

    @pl.loop(1, chips)
    def _(k):
        out_copy(k).wait_send()

    @pl.loop(0, chips)
    def _(k):
        pass_copy(k).wait_send()


def refine_x(rows, ox_ref, wx_ref, grid_ref, out_ref):
    comps = grid_ref.shape[0]
    start = pl.program_id(0) * rows

    @pl.loop(0, rows, unroll=4)
    def _(r):
        i = start + r
        first = ox_ref[i]
        weights = [wx_ref[k, i] for k in range(BAND)]
        for c in range(comps):
            acc = weights[0] * grid_ref[c, first]
            for k in range(1, BAND):
                acc = acc + weights[k] * grid_ref[c, first + k]
            out_ref[c, r] = acc


def solution(mesh):
    n = mesh.shape["slab"]
    vmem = pl.BlockSpec(memory_space=pltpu.VMEM)
    smem = pl.BlockSpec(memory_space=pltpu.SMEM)

    def body(points, offsets_x, coeffs_x, offsets_y, coeffs_y, offsets_z, coeffs_z):
        comps, xl, ny, nz = points.shape
        nx = xl * n
        mx, my, mz = offsets_x.shape[0], offsets_y.shape[0], offsets_z.shape[0]
        jl = my // n
        fold = 128 // nz
        pairs = comps * xl // fold
        lanes = fold * nz
        chips = n // 2
        cl = jl // 2
        wide, narrow = 2 * cl + REACH, cl + REACH
        slab = jnp.transpose(points, (0, 1, 3, 2)).reshape(pairs, lanes, ny)
        f32, bf16 = jnp.float32, jnp.bfloat16
        grid, wx = pl.pallas_call(
            functools.partial(exchange, (n, comps, xl, ny, nz, jl, mz)),
            out_shape=(
                jax.ShapeDtypeStruct((comps, nx, jl, mz), f32),
                jax.ShapeDtypeStruct((BAND, mx), f32),
            ),
            in_specs=[vmem, smem, smem, vmem, vmem, vmem],
            out_specs=(vmem, vmem),
            scratch_shapes=[
                pltpu.VMEM((ny * pairs, lanes), f32),
                pltpu.VMEM((chips, wide, pairs, lanes), f32),
                pltpu.VMEM((chips, narrow, pairs, lanes), f32),
                pltpu.VMEM((jl * SPAN, pairs, lanes), f32),
                pltpu.VMEM((2 * lanes, fold * mz), bf16),
                pltpu.VMEM((lanes, fold * mz), bf16),
                pltpu.VMEM((2 * pairs * jl, lanes), f32),
                pltpu.SemaphoreType.DMA((chips,)),
                pltpu.SemaphoreType.DMA((chips,)),
                pltpu.SemaphoreType.DMA((chips,)),
                pltpu.SemaphoreType.DMA((chips,)),
            ],
            compiler_params=pltpu.CompilerParams(collective_id=0, has_side_effects=True),
            name="exchange",
        )(slab, offsets_y, coeffs_y, offsets_z.reshape(1, mz), coeffs_z, coeffs_x)
        steps = 8
        rows = mx // steps
        return pl.pallas_call(
            functools.partial(refine_x, rows),
            out_shape=jax.ShapeDtypeStruct((comps, mx, jl, mz), f32),
            grid=(steps,),
            in_specs=[smem, smem, pl.BlockSpec((comps, nx, jl, mz), lambda s: (0, 0, 0, 0))],
            out_specs=pl.BlockSpec((comps, rows, jl, mz), lambda s: (0, s, 0, 0)),
            name="refine_x",
        )(offsets_x, wx, grid)

    return jax.shard_map(
        body,
        mesh=mesh,
        in_specs=(P(None, "slab", None, None), P(), P(), P(), P(), P(), P()),
        out_specs=P(None, None, "slab", None),
        check_vma=False,
    )
```

time: 67.9 us -> 35.8 us (0.53)
  the two profiles are of different devices: /device:TPU:0 before, /device:TPU:1 now
where the time goes in v1:
time: 35.8 us; the launch traced here: 35.7 us
  Pallas kernels  35.6 us (99%)
    pallas_call x1, Pallas kernels, body(): pl.pallas_call(functools.partial(exchange, (n, comps, xl, ny, nz, jl, mz)...  29.6 us
    pallas_call x1, Pallas kernels, body(): pl.pallas_call(functools.partial(refine_x, rows), out_shape=jax.ShapeDtyp...  6.08 us

profile of v1, /device:TPU:1, one launch (start us, length us, event | category | flops | bytes accessed | tf_op | source)
XLA Modules:
  0.0 35.7 jit_solution(9173838241455820933)
XLA Ops:
  0.0 29.6 %exchange.1 = (f32[4,128,8,128]{3,2,1,0:T(8,128)}, f32[4,256]{1,0:T(4,128)}) custom-call(f32[8,128,128]{2,1,0:T(8,128)} %bitcast.4, s32[256]{0:T(256)} %oy_ref.1, f32[4,256]{1,0:T(4,128)} %cy_ref.1, s32[1,128]{1,0:T(1,128)} %bitcast.5, f32[4,128]{1,0:T(4,128)} %cz_ref.1, f32[4,256]{1,0:T(4,128)} %cx_ref.1), custom_call_target="tpu_custom_call" | custom-call | tf_op jit(solution)/shard_map/exchange/pallas_call | solution.py:222
  29.6 6.1 %refine_x.1 = f32[4,256,8,128]{3,2,1,0:T(8,128)} custom-call(s32[256]{0:T(256)} %ox_ref.1, f32[4,256]{1,0:T(4,128)} %get-tuple-element.7.wx_ref, f32[4,128,8,128]{3,2,1,0:T(8,128)} %get-tuple-element.8.grid_ref), custom_call_target="tpu_custom_call" | custom-call | tf_op jit(solution)/shard_map/refine_x/pallas_call | solution.py:248

commit v2 on v1

--- a/solution.py
+++ b/solution.py
@@ -222,7 +222,7 @@
         grid, wx = pl.pallas_call(
             functools.partial(exchange, (n, comps, xl, ny, nz, jl, mz)),
             out_shape=(
-                jax.ShapeDtypeStruct((comps, nx, jl, mz), f32),
+                pltpu.VMEM((comps, nx, jl, mz), f32),
                 jax.ShapeDtypeStruct((BAND, mx), f32),
             ),
             in_specs=[vmem, smem, smem, vmem, vmem, vmem],
@@ -249,10 +249,10 @@
             functools.partial(refine_x, rows),
             out_shape=jax.ShapeDtypeStruct((comps, mx, jl, mz), f32),
             grid=(steps,),
-            in_specs=[smem, smem, pl.BlockSpec((comps, nx, jl, mz), lambda s: (0, 0, 0, 0))],
+            in_specs=[smem, smem, vmem],
             out_specs=pl.BlockSpec((comps, rows, jl, mz), lambda s: (0, s, 0, 0)),
             name="refine_x",
-        )(offsets_x, wx, grid)
+        )(offsets_x, wx, pltpu.with_memory_space_constraint(grid, pltpu.VMEM))
 
     return jax.shard_map(
         body,

time: 35.8 us -> 34.2 us (0.955)
  Pallas kernels: 35.6 us -> 34 us
    pallas_call x1, Pallas kernels: 6.08 us -> 5.21 us  [body(): pl.pallas_call(functools.partial(refine_x, rows), out_shape=jax.ShapeDtyp...]
    pallas_call x1, Pallas kernels: 29.6 us -> 28.8 us  [body(): pl.pallas_call(functools.partial(exchange, (n, comps, xl, ny, nz, jl, mz)...]
where the time goes in v2:
time: 34.2 us; the launch traced here: 34 us
  Pallas kernels  34 us (99%)
    pallas_call x1, Pallas kernels, body(): pl.pallas_call(functools.partial(exchange, (n, comps, xl, ny, nz, jl, mz)...  28.8 us
    pallas_call x1, Pallas kernels, body(): pl.pallas_call(functools.partial(refine_x, rows), out_shape=jax.ShapeDtyp...  5.21 us

profile of v2, /device:TPU:1, one launch (start us, length us, event | category | flops | bytes accessed | tf_op | source)
XLA Modules:
  0.0 34.0 jit_solution(16984341105005778730)
XLA Ops:
  0.0 28.8 %exchange.1 = (f32[4,128,8,128]{3,2,1,0:T(8,128)S(1)}, f32[4,256]{1,0:T(4,128)}) custom-call(f32[8,128,128]{2,1,0:T(8,128)} %bitcast.4, s32[256]{0:T(256)} %oy_ref.1, f32[4,256]{1,0:T(4,128)} %cy_ref.1, s32[1,128]{1,0:T(1,128)} %bitcast.5, f32[4,128]{1,0:T(4,128)} %cz_ref.1, f32[4,256]{1,0:T(4,128)} %cx_ref.1), custom_call_target="tpu_custom_call" | custom-call | tf_op jit(solution)/shard_map/exchange/pallas_call | solution.py:222
  28.8 5.2 %refine_x.1 = f32[4,256,8,128]{3,2,1,0:T(8,128)} custom-call(s32[256]{0:T(256)} %ox_ref.1, f32[4,256]{1,0:T(4,128)} %get-tuple-element.7.wx_ref, f32[4,128,8,128]{3,2,1,0:T(8,128)S(1)} %get-tuple-element.8.grid_ref), custom_call_target="tpu_custom_call" | custom-call | tf_op jit(solution)/shard_map/refine_x/pallas_call | solution.py:248

commit v3 on v2

v3 whole, which is shorter than its diff:
```python
import functools

import jax
import jax.numpy as jnp
from jax import lax
from jax.experimental import pallas as pl
from jax.experimental.pallas import tpu as pltpu
from jax.sharding import PartitionSpec as P

MESH = pl.DeviceIdType.MESH
BAND = 4
REACH = BAND + 1
SPAN = BAND + 2
BELOW, ABOVE = 2, 3
PLANES = 4


def flip(a, k, chips):
    out = 0
    bit = 1
    while bit < chips:
        a_bit, k_bit = (a // bit) % 2, (k // bit) % 2
        out = out + (a_bit + k_bit - 2 * a_bit * k_bit) * bit
        bit *= 2
    return out


def span_of(me, jl, ny, j):
    return jnp.clip((me * jl + j) // 2 - 2, 0, ny - SPAN)


def make_weights(dims, me, span_base, oy_ref, cy_ref, oz_ref, cz_ref, cx_ref, wx_ref, wy, rz, rz_lo):
    n, comps, xl, ny, nz, jl, mz = dims
    pairs, lanes = wy.shape[1], wy.shape[2]
    fold = lanes // nz
    wx_ref[...] = cx_ref[...] / jnp.sum(cx_ref[...], axis=0, keepdims=True)
    wz = cz_ref[...] / jnp.sum(cz_ref[...], axis=0, keepdims=True)
    at = lax.broadcasted_iota(jnp.int32, (nz, mz), 0)
    first = jnp.broadcast_to(oz_ref[...], (nz, mz))
    band = jnp.zeros((nz, mz), jnp.float32)
    for k in range(BAND):
        band = band + jnp.where(at == first + k, jnp.broadcast_to(wz[k : k + 1], (nz, mz)), 0.0)
    high = band.astype(jnp.bfloat16)
    low = (band - high.astype(jnp.float32)).astype(jnp.bfloat16)
    rz[...] = jnp.zeros_like(rz)
    rz_lo[...] = jnp.zeros_like(rz_lo)
    for f in range(fold):
        rz[f * nz : (f + 1) * nz, f * mz : (f + 1) * mz] = high
        rz[lanes + f * nz : lanes + (f + 1) * nz, f * mz : (f + 1) * mz] = high
        rz_lo[f * nz : (f + 1) * nz, f * mz : (f + 1) * mz] = low
    for j in range(jl):
        coeffs = [jnp.full((pairs, lanes), cy_ref[k, me * jl + j]) for k in range(BAND)]
        total = coeffs[0] + coeffs[1] + coeffs[2] + coeffs[3]
        coeffs = [c / total for c in coeffs]
        skip = jnp.full((pairs, lanes), oy_ref[me * jl + j] - span_base(j))
        for m in range(SPAN):
            weight = jnp.zeros((pairs, lanes), jnp.float32)
            for k in range(max(0, m - SPAN + BAND), min(BAND, m + 1)):
                weight = jnp.where(skip == m - k, coeffs[k], weight)
            wy[j * SPAN + m] = weight


def refine_y(jl, pairs, span_base, wy, mixed, place, load, base):
    for j in range(jl):
        row = span_base(j) - base
        acc = wy[j * SPAN] * load(row)
        for m in range(1, SPAN):
            acc = acc + wy[j * SPAN + m] * load(row + m)
        mixed[pl.ds(place * pairs * jl + j, pairs, stride=jl), :] = acc


def refine_z(dims, pairs, mixed, rz, rz_lo, grid_ref, devices):
    n, comps, xl, ny, nz, jl, mz = dims
    fold = mixed.shape[1] // nz
    rows = pairs * jl * len(devices)
    x = mixed[:rows]
    hi = x.astype(jnp.bfloat16)
    lo = (x - hi.astype(jnp.float32)).astype(jnp.bfloat16)
    both = jnp.concatenate([hi, lo], axis=1)
    res = jnp.dot(both, rz[...], preferred_element_type=jnp.float32)
    res = res + jnp.dot(hi, rz_lo[...], preferred_element_type=jnp.float32)
    per = pairs // comps
    for q, device in enumerate(devices):
        for p in range(pairs):
            for f in range(fold):
                spot = (p // per, device * xl + (p % per) * fold + f)
                top = (q * pairs + p) * jl
                grid_ref[spot] = res[top : top + jl, f * mz : (f + 1) * mz]


def exchange(
    dims,
    points_ref, oy_ref, cy_ref, oz_ref, cz_ref, cx_ref,
    grid_ref, wx_ref,
    send, direct, passed, wy, rz, rz_lo, mixed,
    send_sem, recv_sem, pass_send_sem, pass_recv_sem,
):
    n, comps, xl, ny, nz, jl, mz = dims
    chips = n // 2
    pairs, lanes = points_ref.shape[0], points_ref.shape[1]
    cl = jl // 2
    wide, narrow = 2 * cl + REACH, cl + REACH
    me = lax.axis_index("slab")
    chip, core = me // 2, me % 2
    partner = chip * 2 + 1 - core

    def wide_base(c):
        return jnp.clip(c * 2 * cl - 2, 0, ny - wide)

    def narrow_base(d):
        return jnp.clip(d * cl - 2, 0, ny - narrow)

    span_base = functools.partial(span_of, me, jl, ny)

    rows_of_y = send.reshape(ny, pairs, lanes)

    barrier = pltpu.get_barrier_semaphore()
    pl.semaphore_signal(barrier, inc=1, device_id=(partner,), device_id_type=MESH)

    @pl.loop(1, chips)
    def _(k):
        other = flip(chip, k, chips) * 2 + core
        pl.semaphore_signal(barrier, inc=1, device_id=(other,), device_id_type=MESH)

    for p in range(pairs):
        send[pl.ds(p, ny, stride=pairs), :] = points_ref[p].T

    pl.semaphore_wait(barrier, chips)

    def out_copy(k):
        target = flip(chip, k, chips)
        return pltpu.make_async_remote_copy(
            src_ref=rows_of_y.at[pl.ds(wide_base(target), wide)],
            dst_ref=direct.at[k],
            send_sem=send_sem.at[k],
            recv_sem=recv_sem.at[k],
            device_id=(target * 2 + core,),
            device_id_type=MESH,
        )

    def pass_copy(k):
        skip = narrow_base(partner) - wide_base(chip)
        return pltpu.make_async_remote_copy(
            src_ref=direct.at[k, pl.ds(skip, narrow)],
            dst_ref=passed.at[k],
            send_sem=pass_send_sem.at[k],
            recv_sem=pass_recv_sem.at[k],
            device_id=(partner,),
            device_id_type=MESH,
        )

    @pl.loop(1, chips)
    def _(k):
        out_copy(k).start()

    own = pl.ds(wide_base(chip), wide)
    stay = pltpu.make_async_copy(rows_of_y.at[own], direct.at[0], recv_sem.at[0])
    stay.start()

    make_weights(dims, me, span_base, oy_ref, cy_ref, oz_ref, cz_ref, cx_ref, wx_ref, wy, rz, rz_lo)

    def from_direct(place, k):
        refine_y(
            jl, pairs, span_base, wy, mixed, place,
            lambda row: direct[k, row],
            wide_base(chip),
        )
        return flip(chip, k, chips) * 2 + core

    def from_passed(place, k):
        refine_y(
            jl, pairs, span_base, wy, mixed, place,
            lambda row: passed[k, row],
            narrow_base(me),
        )
        return flip(chip, k, chips) * 2 + 1 - core

    stay.wait()
    pass_copy(0).start()
    refine_z(dims, pairs, mixed, rz, rz_lo, grid_ref, [from_direct(0, 0)])

    @pl.loop(1, chips)
    def _(k):
        out_copy(k).wait_recv()
        pass_copy(k).start()
        one = from_direct(0, k)
        pass_copy(k - 1).wait_recv()
        two = from_passed(1, k - 1)
        refine_z(dims, pairs, mixed, rz, rz_lo, grid_ref, [one, two])

    pass_copy(chips - 1).wait_recv()
    refine_z(dims, pairs, mixed, rz, rz_lo, grid_ref, [from_passed(0, chips - 1)])

    @pl.loop(1, chips)
    def _(k):
        out_copy(k).wait_send()

    @pl.loop(0, chips)
    def _(k):
        pass_copy(k).wait_send()


def relay(
    dims,
    points_ref, oy_ref, cy_ref, oz_ref, cz_ref, cx_ref,
    grid_ref, wx_ref,
    send, held, wy, rz, rz_lo, mixed,
    main_send, main_recv, pass_send, pass_recv, up_send, down_send, halo_recv, edge_send,
):
    n, comps, xl, ny, nz, jl, mz = dims
    chips = n // 2
    plane = chips // PLANES
    pairs, lanes = points_ref.shape[0], points_ref.shape[1]
    own = jl
    me = lax.axis_index("slab")
    chip, core = me // 2, me % 2
    partner = chip * 2 + 1 - core
    here, level = chip % plane, chip // plane
    middle = pl.ds(BELOW, own)
    rows_of_y = send.reshape(ny, pairs, lanes)

    barrier = pltpu.get_barrier_semaphore()

    @pl.loop(1, n)
    def _(k):
        pl.semaphore_signal(barrier, inc=1, device_id=((me + k) % n,), device_id_type=MESH)

    for p in range(pairs):
        send[pl.ds(p, ny, stride=pairs), :] = points_ref[p].T
    span_base = functools.partial(span_of, me, jl, ny)
    make_weights(dims, me, span_base, oy_ref, cy_ref, oz_ref, cz_ref, cx_ref, wx_ref, wy, rz, rz_lo)
    held[me, middle] = rows_of_y[pl.ds(chip * own, own)]

    pl.semaphore_wait(barrier, n - 1)

    def remote(src, dst, send_sem, recv_sem, device):
        return pltpu.make_async_remote_copy(
            src_ref=src, dst_ref=dst, send_sem=send_sem, recv_sem=recv_sem,
            device_id=(device,), device_id_type=MESH,
        )

    def main_copy(k):
        target = flip(chip, k, chips)
        return remote(
            rows_of_y.at[pl.ds(target * own, own)], held.at[me, middle],
            main_send.at[k], main_recv.at[k], target * 2 + core,
        )

    def main_arrival(k):
        source = flip(chip, k, chips) * 2 + core
        return remote(held.at[source, middle], held.at[source, middle], main_send.at[k], main_recv.at[k], partner)

    def pass_copy(k):
        source = flip(chip, k, chips) * 2 + core
        return remote(held.at[source, middle], held.at[source, middle], pass_send.at[k], pass_recv.at[k], partner)

    def pass_arrival(k):
        source = flip(chip, k, chips) * 2 + 1 - core
        return remote(held.at[source, middle], held.at[source, middle], pass_send.at[k], pass_recv.at[k], partner)

    def up_copy(k):
        source = flip(chip, k, chips) * 2 + core
        return remote(
            held.at[source, pl.ds(own, BELOW)], held.at[source, pl.ds(0, BELOW)],
            up_send.at[k], halo_recv.at[source], chip * 2 + 2,
        )

    def down_copy(k):
        source = flip(chip, k, chips) * 2 + core
        return remote(
            held.at[source, pl.ds(BELOW, ABOVE)], held.at[source, pl.ds(BELOW + own, ABOVE)],
            down_send.at[k], halo_recv.at[source], chip * 2 - 1,
        )

    has_up = here < plane - 1
    has_down = here > 0

    def edge_below(g):
        target = flip(level, g, PLANES) * plane
        copy = lambda: remote(
            rows_of_y.at[pl.ds(target * own - BELOW, BELOW)], held.at[me, pl.ds(0, BELOW)],
            edge_send.at[g], halo_recv.at[me], target * 2,
        )
        return (target > 0) & (target * 2 != me), copy

    def edge_above(g):
        target = flip(level, g, PLANES) * plane + plane - 1
        copy = lambda: remote(
            rows_of_y.at[pl.ds(target * own + own, ABOVE)], held.at[me, pl.ds(BELOW + own, ABOVE)],
            edge_send.at[PLANES + g], halo_recv.at[me], target * 2 + 1,
        )
        return (target < chips - 1) & (target * 2 + 1 != me), copy

    def send_edges(g):
        for edge in (edge_below, edge_above):
            needed, copy = edge(g)

            @pl.when(needed)
            def _():
                copy().start()

    def hand_on(k):
        pass_copy(k).start()

        @pl.when(has_up)
        def _():
            up_copy(k).start()

        @pl.when(has_down)
        def _():
            down_copy(k).start()

    @pl.loop(1, plane)
    def _(k):
        main_copy(k).start()

    send_edges(0)
    hand_on(0)

    for g in range(1, PLANES):

        @pl.loop(g * plane, (g + 1) * plane)
        def _(k):
            main_copy(k).start()

        send_edges(g)

    at_bottom = (here == 0) & (core == 0)
    at_top = (here == plane - 1) & (core == 1)

    @pl.when(at_bottom & (chip > 0))
    def _():
        held[me, 0:BELOW] = rows_of_y[pl.ds(chip * own - BELOW, BELOW)]

    @pl.when(at_top & (chip < chips - 1))
    def _():
        held[me, BELOW + own :] = rows_of_y[pl.ds(chip * own + own, ABOVE)]

    def await_halo(source):
        away = (source != me) | ((here != 0) & (core == 0)) | ((here != plane - 1) & (core == 1))

        @pl.when(away & (core == 0) & (chip > 0))
        def _():
            rows = held.at[source, pl.ds(0, BELOW)]
            remote(rows, rows, up_send.at[0], halo_recv.at[source], partner).wait_recv()

        @pl.when(away & (core == 1) & (chip < chips - 1))
        def _():
            rows = held.at[source, pl.ds(BELOW + own, ABOVE)]
            remote(rows, rows, up_send.at[0], halo_recv.at[source], partner).wait_recv()

    def refine(k):
        other = flip(chip, k, chips) * 2
        pass_arrival(k).wait_recv()
        for c in range(2):
            await_halo(other + c)
        for c in range(2):
            refine_y(jl, pairs, span_base, wy, mixed, c, lambda row: held[other + c, row], chip * own - BELOW)
        refine_z(dims, pairs, mixed, rz, rz_lo, grid_ref, [other, other + 1])

    @pl.loop(1, plane)
    def _(k):
        main_arrival(k).wait_recv()
        hand_on(k)

    @pl.loop(1, PLANES)
    def _(g):
        @pl.loop(0, plane)
        def _(r):
            main_arrival(g * plane + r).wait_recv()
            hand_on(g * plane + r)

        @pl.loop(0, plane)
        def _(r):
            refine((g - 1) * plane + r)

    @pl.loop(0, plane)
    def _(r):
        refine((PLANES - 1) * plane + r)

    @pl.loop(1, chips)
    def _(k):
        main_copy(k).wait_send()

    @pl.loop(0, chips)
    def _(k):
        pass_copy(k).wait_send()

        @pl.when(has_up)
        def _():
            up_copy(k).wait_send()

        @pl.when(has_down)
        def _():
            down_copy(k).wait_send()

    for g in range(PLANES):
        for edge in (edge_below, edge_above):
            needed, copy = edge(g)

            @pl.when(needed)
            def _():
                copy().wait_send()


def refine_x(rows, ox_ref, wx_ref, grid_ref, out_ref):
    comps = grid_ref.shape[0]
    start = pl.program_id(0) * rows

    @pl.loop(0, rows, unroll=4)
    def _(r):
        i = start + r
        first = ox_ref[i]
        weights = [wx_ref[k, i] for k in range(BAND)]
        for c in range(comps):
            acc = weights[0] * grid_ref[c, first]
            for k in range(1, BAND):
                acc = acc + weights[k] * grid_ref[c, first + k]
            out_ref[c, r] = acc


def solution(mesh):
    n = mesh.shape["slab"]
    vmem = pl.BlockSpec(memory_space=pltpu.VMEM)
    smem = pl.BlockSpec(memory_space=pltpu.SMEM)

    def body(points, offsets_x, coeffs_x, offsets_y, coeffs_y, offsets_z, coeffs_z):
        comps, xl, ny, nz = points.shape
        nx = xl * n
        mx, my, mz = offsets_x.shape[0], offsets_y.shape[0], offsets_z.shape[0]
        jl = my // n
        fold = 128 // nz
        pairs = comps * xl // fold
        lanes = fold * nz
        chips = n // 2
        cl = jl // 2
        wide, narrow = 2 * cl + REACH, cl + REACH
        slab = jnp.transpose(points, (0, 1, 3, 2)).reshape(pairs, lanes, ny)
        f32, bf16 = jnp.float32, jnp.bfloat16
        if jl >= ABOVE and chips % PLANES == 0:
            kernel, name = relay, "relay"
            buffers = [pltpu.VMEM((n, BELOW + jl + ABOVE, pairs, lanes), f32)]
            counts = [chips] * 6 + [n, 2 * PLANES]
        else:
            kernel, name = exchange, "exchange"
            buffers = [
                pltpu.VMEM((chips, wide, pairs, lanes), f32),
                pltpu.VMEM((chips, narrow, pairs, lanes), f32),
            ]
            counts = [chips] * 4
        grid, wx = pl.pallas_call(
            functools.partial(kernel, (n, comps, xl, ny, nz, jl, mz)),
            out_shape=(
                pltpu.VMEM((comps, nx, jl, mz), f32),
                jax.ShapeDtypeStruct((BAND, mx), f32),
            ),
            in_specs=[vmem, smem, smem, vmem, vmem, vmem],
            out_specs=(vmem, vmem),
            scratch_shapes=[
                pltpu.VMEM((ny * pairs, lanes), f32),
                *buffers,
                pltpu.VMEM((jl * SPAN, pairs, lanes), f32),
                pltpu.VMEM((2 * lanes, fold * mz), bf16),
                pltpu.VMEM((lanes, fold * mz), bf16),
                pltpu.VMEM((2 * pairs * jl, lanes), f32),
                *[pltpu.SemaphoreType.DMA((count,)) for count in counts],
            ],
            compiler_params=pltpu.CompilerParams(collective_id=0, has_side_effects=True),
            name=name,
        )(slab, offsets_y, coeffs_y, offsets_z.reshape(1, mz), coeffs_z, coeffs_x)
        steps = 8
        rows = mx // steps
        return pl.pallas_call(
            functools.partial(refine_x, rows),
            out_shape=jax.ShapeDtypeStruct((comps, mx, jl, mz), f32),
            grid=(steps,),
            in_specs=[smem, smem, vmem],
            out_specs=pl.BlockSpec((comps, rows, jl, mz), lambda s: (0, s, 0, 0)),
            name="refine_x",
        )(offsets_x, wx, pltpu.with_memory_space_constraint(grid, pltpu.VMEM))

    return jax.shard_map(
        body,
        mesh=mesh,
        in_specs=(P(None, "slab", None, None), P(), P(), P(), P(), P(), P()),
        out_specs=P(None, None, "slab", None),
        check_vma=False,
    )
```

time: 34.2 us -> 31.6 us (0.924)
  Pallas kernels: 34 us -> 31.4 us
    pallas_call x1, Pallas kernels: 28.8 us -> 26.2 us  [body(): pl.pallas_call(functools.partial(kernel, (n, comps, xl, ny, nz, jl, mz)),...]
where the time goes in v3:
time: 31.6 us; the launch traced here: 31.4 us
  Pallas kernels  31.4 us (99%)
    pallas_call x1, Pallas kernels, body(): pl.pallas_call(functools.partial(kernel, (n, comps, xl, ny, nz, jl, mz)),...  26.2 us
    pallas_call x1, Pallas kernels, body(): pl.pallas_call(functools.partial(refine_x, rows), out_shape=jax.ShapeDtyp...  5.21 us

profile of v3, /device:TPU:1, one launch (start us, length us, event | category | flops | bytes accessed | tf_op | source)
XLA Modules:
  0.0 31.4 jit_solution(15132137064208864207)
XLA Ops:
  0.0 26.2 %relay.1 = (f32[4,128,8,128]{3,2,1,0:T(8,128)S(1)}, f32[4,256]{1,0:T(4,128)}) custom-call(f32[8,128,128]{2,1,0:T(8,128)} %bitcast.4, s32[256]{0:T(256)} %oy_ref.1, f32[4,256]{1,0:T(4,128)} %cy_ref.1, s32[1,128]{1,0:T(1,128)} %bitcast.5, f32[4,128]{1,0:T(4,128)} %cz_ref.1, f32[4,256]{1,0:T(4,128)} %cx_ref.1), custom_call_target="tpu_custom_call" | custom-call | tf_op jit(solution)/shard_map/relay/pallas_call | solution.py:451
  26.2 5.2 %refine_x.1 = f32[4,256,8,128]{3,2,1,0:T(8,128)} custom-call(s32[256]{0:T(256)} %ox_ref.1, f32[4,256]{1,0:T(4,128)} %get-tuple-element.7.wx_ref, f32[4,128,8,128]{3,2,1,0:T(8,128)S(1)} %get-tuple-element.8.grid_ref), custom_call_target="tpu_custom_call" | custom-call | tf_op jit(solution)/shard_map/refine_x/pallas_call | solution.py:473

commit v4 on v3

--- a/solution.py
+++ b/solution.py
@@ -13,6 +13,7 @@
 SPAN = BAND + 2
 BELOW, ABOVE = 2, 3
 PLANES = 4
+GROUP = 8
 
 
 def flip(a, k, chips):
@@ -350,33 +351,41 @@
             remote(rows, rows, up_send.at[0], halo_recv.at[source], partner).wait_recv()
 
     def refine(k):
-        other = flip(chip, k, chips) * 2
-        pass_arrival(k).wait_recv()
-        for c in range(2):
-            await_halo(other + c)
-        for c in range(2):
-            refine_y(jl, pairs, span_base, wy, mixed, c, lambda row: held[other + c, row], chip * own - BELOW)
-        refine_z(dims, pairs, mixed, rz, rz_lo, grid_ref, [other, other + 1])
-
-    @pl.loop(1, plane)
-    def _(k):
+        others = [flip(chip, k + i, chips) * 2 for i in range(2)]
+        for i in range(2):
+            pass_arrival(k + i).wait_recv()
+        devices = [other + c for other in others for c in range(2)]
+        for device in devices:
+            await_halo(device)
+        for j in range(jl):
+            row = span_base(j) - (chip * own - BELOW)
+            sums = [None] * len(devices)
+            for m in range(SPAN):
+                weight = wy[j * SPAN + m]
+                for i, device in enumerate(devices):
+                    term = weight * held[device, row + m]
+                    sums[i] = term if m == 0 else sums[i] + term
+            for i, total in enumerate(sums):
+                mixed[pl.ds(i * pairs * jl + j, pairs, stride=jl), :] = total
+        refine_z(dims, pairs, mixed, rz, rz_lo, grid_ref, devices)
+
+    def take(k):
         main_arrival(k).wait_recv()
         hand_on(k)
 
-    @pl.loop(1, PLANES)
-    def _(g):
-        @pl.loop(0, plane)
-        def _(r):
-            main_arrival(g * plane + r).wait_recv()
-            hand_on(g * plane + r)
-
-        @pl.loop(0, plane)
-        def _(r):
-            refine((g - 1) * plane + r)
-
-    @pl.loop(0, plane)
-    def _(r):
-        refine((PLANES - 1) * plane + r)
+    @pl.loop(1, plane)
+    def _(k):
+        take(k)
+
+    @pl.loop(plane // 2, chips // 2)
+    def _(h):
+        take(2 * h)
+        take(2 * h + 1)
+        refine(2 * h - plane)
+
+    @pl.loop((chips - plane) // 2, chips // 2)
+    def _(h):
+        refine(2 * h)
 
     @pl.loop(1, chips)
     def _(k):
@@ -403,20 +412,36 @@
                 copy().wait_send()
 
 
-def refine_x(rows, ox_ref, wx_ref, grid_ref, out_ref):
-    comps = grid_ref.shape[0]
-    start = pl.program_id(0) * rows
-
-    @pl.loop(0, rows, unroll=4)
-    def _(r):
-        i = start + r
-        first = ox_ref[i]
-        weights = [wx_ref[k, i] for k in range(BAND)]
-        for c in range(comps):
-            acc = weights[0] * grid_ref[c, first]
-            for k in range(1, BAND):
-                acc = acc + weights[k] * grid_ref[c, first + k]
-            out_ref[c, r] = acc
+def refine_x(steps, ox_ref, wx_ref, grid_ref, out_ref, block, sems):
+    comps, mx = block.shape[0], block.shape[1]
+    rows = mx // steps
+
+    def put(s):
+        part = pl.ds(pl.multiple_of(s * rows, rows), rows)
+        return pltpu.make_async_copy(block.at[:, part], out_ref.at[:, part], sems.at[s])
+
+    @pl.loop(0, steps)
+    def _(s):
+        @pl.loop(0, rows // GROUP)
+        def _(g):
+            done = []
+            for q in range(GROUP):
+                i = s * rows + g * GROUP + q
+                first = ox_ref[i]
+                weights = [wx_ref[k, i] for k in range(BAND)]
+                for c in range(comps):
+                    acc = weights[0] * grid_ref[c, first]
+                    for k in range(1, BAND):
+                        acc = acc + weights[k] * grid_ref[c, first + k]
+                    done.append((c, i, acc))
+            for c, i, acc in done:
+                block[c, i] = acc
+
+        put(s).start()
+
+    @pl.loop(0, steps)
+    def _(s):
+        put(s).wait()
 
 
 def solution(mesh):
@@ -462,20 +487,22 @@
                 pltpu.VMEM((jl * SPAN, pairs, lanes), f32),
                 pltpu.VMEM((2 * lanes, fold * mz), bf16),
                 pltpu.VMEM((lanes, fold * mz), bf16),
-                pltpu.VMEM((2 * pairs * jl, lanes), f32),
+                pltpu.VMEM((4 * pairs * jl, lanes), f32),
                 *[pltpu.SemaphoreType.DMA((count,)) for count in counts],
             ],
             compiler_params=pltpu.CompilerParams(collective_id=0, has_side_effects=True),
             name=name,
         )(slab, offsets_y, coeffs_y, offsets_z.reshape(1, mz), coeffs_z, coeffs_x)
         steps = 8
-        rows = mx // steps
         return pl.pallas_call(
-            functools.partial(refine_x, rows),
+            functools.partial(refine_x, steps),
             out_shape=jax.ShapeDtypeStruct((comps, mx, jl, mz), f32),
-            grid=(steps,),
             in_specs=[smem, smem, vmem],
-            out_specs=pl.BlockSpec((comps, rows, jl, mz), lambda s: (0, s, 0, 0)),
+            out_specs=pl.BlockSpec(memory_space=pltpu.HBM),
+            scratch_shapes=[
+                pltpu.VMEM((comps, mx, jl, mz), f32),
+                pltpu.SemaphoreType.DMA((steps,)),
+            ],
             name="refine_x",
         )(offsets_x, wx, pltpu.with_memory_space_constraint(grid, pltpu.VMEM))
 

time: 31.6 us -> 32 us (1.013)
  Pallas kernels: 31.4 us -> 31.8 us
    pallas_call x1, Pallas kernels: 26.2 us -> 28.6 us  [body(): pl.pallas_call(functools.partial(kernel, (n, comps, xl, ny, nz, jl, mz)),...]
    pallas_call x1, Pallas kernels: 5.21 us -> 3.19 us  [body(): pl.pallas_call(functools.partial(refine_x, steps), out_shape=jax.ShapeDty...]
where the time goes in v4:
time: 32 us; the launch traced here: 31.8 us
  Pallas kernels  31.8 us (99%)
    pallas_call x1, Pallas kernels, body(): pl.pallas_call(functools.partial(kernel, (n, comps, xl, ny, nz, jl, mz)),...  28.6 us
    pallas_call x1, Pallas kernels, body(): pl.pallas_call(functools.partial(refine_x, steps), out_shape=jax.ShapeDty...  3.19 us

profile of v4, /device:TPU:1, one launch (start us, length us, event | category | flops | bytes accessed | tf_op | source)
XLA Modules:
  0.0 31.8 jit_solution(17135464052824026093)
XLA Ops:
  0.0 28.6 %relay.1 = (f32[4,128,8,128]{3,2,1,0:T(8,128)S(1)}, f32[4,256]{1,0:T(4,128)}) custom-call(f32[8,128,128]{2,1,0:T(8,128)} %bitcast.4, s32[256]{0:T(256)} %oy_ref.1, f32[4,256]{1,0:T(4,128)} %cy_ref.1, s32[1,128]{1,0:T(1,128)} %bitcast.5, f32[4,128]{1,0:T(4,128)} %cz_ref.1, f32[4,256]{1,0:T(4,128)} %cx_ref.1), custom_call_target="tpu_custom_call" | custom-call | tf_op jit(solution)/shard_map/relay/pallas_call | solution.py:476
  28.6 3.2 %refine_x.1 = f32[4,256,8,128]{3,2,1,0:T(8,128)} custom-call(s32[256]{0:T(256)} %ox_ref.1, f32[4,256]{1,0:T(4,128)} %get-tuple-element.7.wx_ref, f32[4,128,8,128]{3,2,1,0:T(8,128)S(1)} %get-tuple-element.8.grid_ref), custom_call_target="tpu_custom_call" | custom-call | tf_op jit(solution)/shard_map/refine_x/pallas_call | solution.py:497

commit v5 on v4

--- a/solution.py
+++ b/solution.py
@@ -377,11 +377,15 @@
     def _(k):
         take(k)
 
-    @pl.loop(plane // 2, chips // 2)
-    def _(h):
-        take(2 * h)
-        take(2 * h + 1)
-        refine(2 * h - plane)
+    @pl.loop(1, PLANES)
+    def _(g):
+        @pl.loop(0, plane)
+        def _(r):
+            take(g * plane + r)
+
+        @pl.loop(0, plane // 2)
+        def _(h):
+            refine((g - 1) * plane + 2 * h)
 
     @pl.loop((chips - plane) // 2, chips // 2)
     def _(h):

time: 32 us -> 29.2 us (0.912)
  Pallas kernels: 31.8 us -> 28.9 us
    pallas_call x1, Pallas kernels: 28.6 us -> 25.7 us  [body(): pl.pallas_call(functools.partial(kernel, (n, comps, xl, ny, nz, jl, mz)),...]
where the time goes in v5:
time: 29.2 us; the launch traced here: 28.9 us
  Pallas kernels  28.9 us (99%)
    pallas_call x1, Pallas kernels, body(): pl.pallas_call(functools.partial(kernel, (n, comps, xl, ny, nz, jl, mz)),...  25.7 us
    pallas_call x1, Pallas kernels, body(): pl.pallas_call(functools.partial(refine_x, steps), out_shape=jax.ShapeDty...  3.19 us

profile of v5, /device:TPU:1, one launch (start us, length us, event | category | flops | bytes accessed | tf_op | source)
XLA Modules:
  0.0 28.9 jit_solution(17154303536550822255)
XLA Ops:
  0.0 25.7 %relay.1 = (f32[4,128,8,128]{3,2,1,0:T(8,128)S(1)}, f32[4,256]{1,0:T(4,128)}) custom-call(f32[8,128,128]{2,1,0:T(8,128)} %bitcast.4, s32[256]{0:T(256)} %oy_ref.1, f32[4,256]{1,0:T(4,128)} %cy_ref.1, s32[1,128]{1,0:T(1,128)} %bitcast.5, f32[4,128]{1,0:T(4,128)} %cz_ref.1, f32[4,256]{1,0:T(4,128)} %cx_ref.1), custom_call_target="tpu_custom_call" | custom-call | tf_op jit(solution)/shard_map/relay/pallas_call | solution.py:480
  25.7 3.2 %refine_x.1 = f32[4,256,8,128]{3,2,1,0:T(8,128)} custom-call(s32[256]{0:T(256)} %ox_ref.1, f32[4,256]{1,0:T(4,128)} %get-tuple-element.7.wx_ref, f32[4,128,8,128]{3,2,1,0:T(8,128)S(1)} %get-tuple-element.8.grid_ref), custom_call_target="tpu_custom_call" | custom-call | tf_op jit(solution)/shard_map/refine_x/pallas_call | solution.py:501
